TPU v7x, 8 devices: a whole 2x2x1 slice. The times are simulated.
8 devices in a mesh: dp: 1 (over z), tp: 2 (over y), sp: 4 (over x, core).
Axes of the slice: x: 2, y: 2, z: 1, core: 2. Of those that a mesh axis runs over, the one named last changes fastest.
Arguments:
- x_seq: bfloat16 [6144, 2304], P(('dp', 'sp', 'tp'))
- w_query: bfloat16 [2304, 8, 256], P(None, 'tp')
- w_key: bfloat16 [2304, 4, 256], P(None, 'tp')
- w_value: bfloat16 [2304, 4, 256], P(None, 'tp')
- w_out: bfloat16 [8, 256, 2304], P('tp')
Outputs:
- output: bfloat16 [6144, 2304], P(('dp', 'sp', 'tp'))
All inputs are finite; a program needn't handle non-finite values.
Results may differ from a plain program's by a relative error of at most 0.00556017.
Values are sent between devices in bfloat16 or wider.
A program may use at most 1 GiB of HBM per device.

v0:
```python
import jax
import jax.numpy as jnp
from jax import lax
from jax.sharding import PartitionSpec as P

WINDOW = 4096
NEG_BIG = -1e30


def block_update(soft_state, q_blk, k_blk, v_blk, chunk_gap, score_scale):
    row_max, row_sum, acc_sum = soft_state
    chunk_len = q_blk.shape[0]
    scores = jnp.einsum("qhgd,khd->hgqk", q_blk, k_blk, preferred_element_type=jnp.float32) * score_scale
    offset = chunk_gap * chunk_len + lax.broadcasted_iota(jnp.int32, (chunk_len, chunk_len), 0) - lax.broadcasted_iota(jnp.int32, (chunk_len, chunk_len), 1)
    visible = (offset >= 0) & (offset < WINDOW)
    scores = jnp.where(visible, scores, NEG_BIG)
    new_max = jnp.maximum(row_max, jnp.max(scores, axis=-1))
    prob_blk = jnp.where(visible, jnp.exp(scores - new_max[..., None]), 0.0)
    rescale = jnp.exp(row_max - new_max)
    new_sum = row_sum * rescale + jnp.sum(prob_blk, axis=-1)
    new_acc = acc_sum * rescale[..., None] + jnp.einsum("hgqk,khd->hgqd", prob_blk.astype(jnp.bfloat16), v_blk, preferred_element_type=jnp.float32)
    return new_max, new_sum, new_acc


def pair_update(soft_state, q_blk, k_blk, v_blk, q_id, k_id, score_scale):
    chunk_len = q_blk.shape[0]
    chunk_gap = q_id - k_id
    needed = (chunk_gap >= 0) & (chunk_gap * chunk_len - chunk_len + 1 < WINDOW)
    return lax.cond(needed, lambda cur_state: block_update(cur_state, q_blk, k_blk, v_blk, chunk_gap, score_scale), lambda cur_state: cur_state, soft_state)


def solution(mesh):
    sp_size = mesh.shape["sp"]
    next_pairs = [(src_idx, (src_idx + 1) % sp_size) for src_idx in range(sp_size)]

    def local_attn(x_part, w_query, w_key, w_value, w_out):
        x_block = lax.all_gather(x_part, "tp", axis=0, tiled=True)
        block_rows, d_model = x_block.shape
        chunk_len = block_rows // 2
        heads_loc, head_dim = w_query.shape[1], w_query.shape[2]
        kv_loc = w_key.shape[1]
        group_size = heads_loc // kv_loc
        score_scale = head_dim ** -0.5
        q_loc = jnp.dot(x_block, w_query.reshape(d_model, heads_loc * head_dim), preferred_element_type=jnp.float32).astype(jnp.bfloat16).reshape(2, chunk_len, kv_loc, group_size, head_dim)
        k_loc = jnp.dot(x_block, w_key.reshape(d_model, kv_loc * head_dim), preferred_element_type=jnp.float32).astype(jnp.bfloat16).reshape(2, chunk_len, kv_loc, head_dim)
        v_loc = jnp.dot(x_block, w_value.reshape(d_model, kv_loc * head_dim), preferred_element_type=jnp.float32).astype(jnp.bfloat16).reshape(2, chunk_len, kv_loc, head_dim)
        sp_rank = lax.axis_index("sp")
        own_ids = (sp_rank, 2 * sp_size - 1 - sp_rank)

        def fresh_state():
            return (jnp.full((kv_loc, group_size, chunk_len), NEG_BIG, jnp.float32), jnp.zeros((kv_loc, group_size, chunk_len), jnp.float32), jnp.zeros((kv_loc, group_size, chunk_len, head_dim), jnp.float32))

        def absorb(states, k_blocks, v_blocks, src_rank):
            key_ids = (src_rank, 2 * sp_size - 1 - src_rank)
            updated = []
            for q_half in range(2):
                cur_state = states[q_half]
                for k_half in range(2):
                    cur_state = pair_update(cur_state, q_loc[q_half], k_blocks[k_half], v_blocks[k_half], own_ids[q_half], key_ids[k_half], score_scale)
                updated.append(cur_state)
            return tuple(updated)

        states = absorb((fresh_state(), fresh_state()), k_loc, v_loc, sp_rank)

        def ring_free_step(step_idx, carry):
            k_blocks, v_blocks, cur_states = carry
            k_blocks, v_blocks = lax.ppermute((k_blocks, v_blocks), "sp", next_pairs)
            src_rank = (sp_rank - step_idx) % sp_size
            return k_blocks, v_blocks, absorb(cur_states, k_blocks, v_blocks, src_rank)

        carry_out = lax.fori_loop(1, sp_size, ring_free_step, (k_loc, v_loc, states))
        states = carry_out[2]
        outs_norm = jnp.stack([(soft_state[2] / soft_state[1][..., None]).astype(jnp.bfloat16) for soft_state in states])
        part_sum = jnp.einsum("ahgqd,hgde->aqe", outs_norm, w_out.reshape(kv_loc, group_size, head_dim, d_model), preferred_element_type=jnp.float32).reshape(block_rows, d_model)
        y_rows = lax.psum_scatter(part_sum, "tp", scatter_dimension=0, tiled=True)
        return y_rows.astype(jnp.bfloat16)

    return jax.shard_map(local_attn, mesh=mesh, in_specs=(P(("dp", "sp", "tp"), None), P(None, "tp", None), P(None, "tp", None), P(None, "tp", None), P("tp", None, None)), out_specs=P(("dp", "sp", "tp"), None), check_vma=False)
```

profile of v0, /device:TPU:2, one launch (start us, length us, event | category | flops | bytes accessed | tf_op | source)
XLA Modules:
  0.0 598.8 jit_solution(14257213490462216129)
XLA Ops:
  7.3 6.2 %copy.78 = bf16[288,8,4,256]{3,1,2,0:T(8,128)(2,1)} copy(bf16[288,8,4,256]{3,2,1,0:T(4,128)(2,1)} %bitcast.263) | data formatting | bytes 9437184
  18.7 78.3 %all-gather.2.cloned.1.call-done = bf16[1536,2304]{1,0:T(8,128)(2,1)} async-done(((bf16[768,2304]{1,0:T(8,128)(2,1)}), bf16[1536,2304]{1,0:T(8,128)(2,1)}) %all-gather.2.cloned.1.call-update) | async-done | bytes 7077904 | tf_op jit(solution)/shard_map/all_gather | solution.py:37
  97.1 11.6 %convolution_convert_fusion = bf16[1536,1024]{0,1:T(8,128)(2,1)S(1)} fusion(bf16[1536,2304]{1,0:T(8,128)(2,1)} %all-gather.2.cloned.1.call-done, bf16[2304,1024]{1,0:T(8,128)(2,1)} %bitcast.264), kind=kOutput, calls=%fused_computation.149 | convolution fusion | flops 7249330176 | bytes 14942208 | tf_op jit(solution)/shard_map/dot_general | solution.py:44
  112.3 6.3 %reshape.68 = bf16[2,768,2,2,256]{1,0,4,3,2:T(2,128)(2,1)S(1)} reshape(bf16[1536,1024]{0,1:T(8,128)(2,1)} %copy-done.5) | data formatting | bytes 6291456 | tf_op jit(solution)/shard_map/reshape | solution.py:44
  118.6 7.6 %convolution_convert_fusion.2 = bf16[1536,512]{0,1:T(8,128)(2,1)S(1)} fusion(bf16[1536,2304]{1,0:T(8,128)(2,1)} %all-gather.2.cloned.1.call-done, bf16[2304,512]{1,0:T(8,128)(2,1)} %bitcast.271), kind=kOutput, calls=%fused_computation.155 | convolution fusion | flops 3624665088 | bytes 11010048 | tf_op jit(solution)/shard_map/dot_general | solution.py:45
  133.8 7.6 %convolution_convert_fusion.1 = bf16[1536,512]{0,1:T(8,128)(2,1)S(1)} fusion(bf16[1536,2304]{1,0:T(8,128)(2,1)} %all-gather.2.cloned.1.call-done, bf16[2304,512]{1,0:T(8,128)(2,1)} %bitcast.270), kind=kOutput, calls=%fused_computation.154 | convolution fusion | flops 3624665088 | bytes 11010048 | tf_op jit(solution)/shard_map/dot_general | solution.py:46
  151.6 6.4 %fusion.105 = (f32[2,2,768]{2,1,0:T(2,128)S(1)}, f32[2,2,768]{2,1,0:T(2,128)S(1)}, f32[2,768,768,2]{2,1,3,0:T(8,128)}) fusion(pred[768,768]{0,1:T(8,128)(4,1)S(1)} %copy-done.13, f32[2,768,768,2]{2,1,3,0:T(8,128)S(1)} %fusion.137, bf16[768,2,256,1]{0,2,3,1:T(8,128)(2,1)S(1)} %bitcast.274, bf16[768,2,2,256]{0,3,2,1:T(8,128)(2,1)S(1)} %bitcast.273), kind=kOutput, calls=%fused_computation.139 | convolution fusion | flops 1222109184 | bytes 21848064 | tf_op jit(solution)/shard_map/cond/branch_1_fun/qhgd,khd->hgqk/dot_general | solution.py:13
  174.0 14.1 %conditional.7 = (f32[2,2,768]{2,1,0:T(2,128)}, f32[2,2,768]{2,1,0:T(2,128)S(1)}, f32[2,2,768,256]{3,2,1,0:T(8,128)}) conditional(s32[]{:T(128)} %convert_element_type.111, () %tuple.84, (s32[]{:T(128)}, bf16[768,2,256]{0,2,1:T(8,128)(2,1)S(1)}, bf16[768,2,2,256]{0,3,2,1:T(8,128)(2,1)}, bf16[768,2,256]{0,2,1:T(8,128)(2,1)S(1)}) %tuple.175), branch_computations={%region_6.7_spmd, %region_7.10_spmd} | conditional | flops 2449748736 | bytes 37103656 | solution.py:29
  188.8 9.7 %fusion.109 = (f32[2,2,768]{2,1,0:T(2,128)S(1)}, f32[2,2,768]{2,1,0:T(2,128)S(1)}) fusion(f32[2,768,768,2]{2,1,3,0:T(8,128)} %get-tuple-element.762, f32[2,2,768]{2,1,0:T(2,128)S(1)} %max.19, pred[768,768]{0,1:T(8,128)(4,1)S(1)} %copy-done.14, f32[2,2,768]{2,1,0:T(2,128)S(1)} %broadcast_maximum_fusion.1, f32[2,768,768,2]{2,1,3,0:T(8,128)} %copy-done), kind=kLoop, calls=%fused_computation.143 | loop fusion | flops 23586816 | bytes 19513344 | tf_op jit(solution)/shard_map/cond/branch_1_fun/reduce_sum | solution.py:20
  199.4 9.1 %fusion.120 = f32[2,2,768,256]{3,2,1,0:T(8,128)} fusion(bf16[768,2,256,1]{0,2,3,1:T(8,128)(2,1)S(1)} %bitcast.277, f32[2,768,768,2]{2,1,3,0:T(8,128)} %copy-done, f32[2,2,768]{2,1,0:T(2,128)S(1)} %broadcast_maximum_fusion.1, pred[768,768]{0,1:T(8,128)(4,1)S(1)} %copy-done.14, f32[2,2,768]{2,1,0:T(2,128)S(1)} %get-tuple-element.764), kind=kOutput, calls=%fused_computation.160 | convolution fusion | flops 1220542464 | bytes 13983744 | tf_op jit(solution)/shard_map/cond/branch_1_fun/hgqk,khd->hgqd/dot_general | solution.py:21
  208.5 6.5 %multiply_add_fusion.10 = f32[2,2,768,256]{3,2,1,0:T(8,128)} fusion(f32[2,2,768,256]{3,2,1,0:T(8,128)} %get-tuple-element.666, bf16[768,2,256,1]{0,2,3,1:T(8,128)(2,1)} %bitcast.74, f32[2,768,768,2]{2,1,3,0:T(8,128)S(1)} %bitcast.260, f32[2,2,768]{2,1,0:T(2,128)S(1)} %max.19, pred[768,768]{0,1:T(8,128)(4,1)S(1)} %copy-done.14, ...), kind=kOutput, calls=%fused_computation.153 | convolution fusion | flops 1221328896 | bytes 17129472 | tf_op jit(solution)/shard_map/cond/branch_1_fun/hgqk,khd->hgqd/dot_general | solution.py:21
  215.1 197.3 %while.32 = (s32[]{:T(128)}, bf16[2,768,2,256]{3,1,2,0:T(8,128)(2,1)}, bf16[2,768,2,256]{3,1,2,0:T(8,128)(2,1)}, f32[2,2,768]{2,1,0:T(2,128)S(1)}, f32[2,2,768]{...) while((s32[]{:T(128)}, ...), condition=%wide.region_29.30_spmd, body=%wide.region_12.29_spmd.sunk | while | flops 9802116096 | bytes 205284544 | solution.py:71
  219.3 16.0 %collective-permute-done = bf16[2,768,2,256]{3,1,2,0:T(8,128)(2,1)S(1)} collective-permute-done((bf16[2,768,2,256]{3,1,2,0:T(8,128)(2,1)}, bf16[2,768,2,256]{3,1,2,0:T(8,128)(2,1)S(1)}, u32[]{:S(2)}, u32[]{:S(2)}) %collective-permute-start) | collective-permute-done | bytes 1572896 | tf_op jit(solution)/shard_map/while/body/eval_jaxpr/ppermute | solution.py:67
  236.6 15.6 %collective-permute-done.1 = bf16[2,768,2,256]{3,1,2,0:T(8,128)(2,1)S(1)} collective-permute-done((bf16[2,768,2,256]{3,1,2,0:T(8,128)(2,1)}, bf16[2,768,2,256]{3,1,2,0:T(8,128)(2,1)S(1)}, u32[]{:S(2)}, u32[]{:S(2)}) %collective-permute-start.1) | collective-permute-done | bytes 1572896 | tf_op jit(solution)/shard_map/while/body/eval_jaxpr/ppermute | solution.py:67
  253.4 12.6 %conditional.14 = ((f32[2,2,768]{2,1,0:T(2,128)S(1)}, f32[2,2,768]{2,1,0:T(2,128)S(1)}, f32[2,2,768,256]{3,2,1,0:T(8,128)})) conditional(s32[]{:T(128)} %convert_element_type.164, (f32[2,2,768]{2,1,0:T(2,128)S(1)}, f32[2,2,768]{2,1,0:T(2,128)S(1)}, f32[2,2,768,256]{3,2,1,0:T(8,128)}) %tuple.138, (s32[]{:T(128)}, bf16[768,2,256]{2,0,1:T(8,128)(2,1)}, ...), branch_computations={%region_21.21_spmd, %region_22.0_spmd} | conditional | flops 2450529024 | bytes 43456588 | solution.py:29
  259.9 6.2 %multiply_add_fusion.6 = f32[2,2,768,256]{3,2,1,0:T(8,128)} fusion(f32[2,2,768,256]{3,2,1,0:T(8,128)} %get-tuple-element.617, f32[2,768,768,2]{2,1,3,0:T(8,128)S(1)} %get-tuple-element.745, f32[2,2,768]{2,1,0:T(2,128)S(1)} %max.16, pred[768,768]{0,1:T(8,128)(4,1)S(1)} %fusion.78, f32[2,2,768]{2,1,0:T(2,128)S(1)} %get-tuple-element.731, ...), kind=kOutput, calls=%fused_computation.92 | convolution fusion | flops 1221328896 | bytes 17129472 | tf_op jit(solution)/shard_map/while/body/eval_jaxpr/cond/branch_1_fun/hgqk,khd->hgqd/dot_general | solution.py:21
  266.1 12.6 %conditional.12 = ((f32[2,2,768]{2,1,0:T(2,128)S(1)}, f32[2,2,768]{2,1,0:T(2,128)S(1)}, f32[2,2,768,256]{3,2,1,0:T(8,128)})) conditional(s32[]{:T(128)} %convert_element_type.162, (f32[2,2,768]{2,1,0:T(2,128)S(1)}, f32[2,2,768]{2,1,0:T(2,128)S(1)}, f32[2,2,768,256]{3,2,1,0:T(8,128)}) %tuple.135, (s32[]{:T(128)}, bf16[768,2,256]{2,0,1:T(8,128)(2,1)}, ...), branch_computations={%region_13.13_spmd, %region_14.16_spmd} | conditional | flops 2450529024 | bytes 43456588 | solution.py:29
  272.5 6.2 %multiply_add_fusion.2 = f32[2,2,768,256]{3,2,1,0:T(8,128)} fusion(f32[2,2,768,256]{3,2,1,0:T(8,128)} %get-tuple-element.603, f32[2,768,768,2]{2,1,3,0:T(8,128)S(1)} %get-tuple-element.741, f32[2,2,768]{2,1,0:T(2,128)S(1)} %max.14, pred[768,768]{0,1:T(8,128)(4,1)S(1)} %fusion.44, f32[2,2,768]{2,1,0:T(2,128)S(1)} %get-tuple-element.727, ...), kind=kOutput, calls=%fused_computation.50 | convolution fusion | flops 1221328896 | bytes 17129472 | tf_op jit(solution)/shard_map/while/body/eval_jaxpr/cond/branch_1_fun/hgqk,khd->hgqd/dot_general | solution.py:21
  284.8 16.1 %collective-permute-done = bf16[2,768,2,256]{3,1,2,0:T(8,128)(2,1)S(1)} collective-permute-done((bf16[2,768,2,256]{3,1,2,0:T(8,128)(2,1)}, bf16[2,768,2,256]{3,1,2,0:T(8,128)(2,1)S(1)}, u32[]{:S(2)}, u32[]{:S(2)}) %collective-permute-start) | collective-permute-done | bytes 1572896 | tf_op jit(solution)/shard_map/while/body/eval_jaxpr/ppermute | solution.py:67
  302.2 15.6 %collective-permute-done.1 = bf16[2,768,2,256]{3,1,2,0:T(8,128)(2,1)S(1)} collective-permute-done((bf16[2,768,2,256]{3,1,2,0:T(8,128)(2,1)}, bf16[2,768,2,256]{3,1,2,0:T(8,128)(2,1)S(1)}, u32[]{:S(2)}, u32[]{:S(2)}) %collective-permute-start.1) | collective-permute-done | bytes 1572896 | tf_op jit(solution)/shard_map/while/body/eval_jaxpr/ppermute | solution.py:67
  319.0 12.6 %conditional.14 = ((f32[2,2,768]{2,1,0:T(2,128)S(1)}, f32[2,2,768]{2,1,0:T(2,128)S(1)}, f32[2,2,768,256]{3,2,1,0:T(8,128)})) conditional(s32[]{:T(128)} %convert_element_type.164, (f32[2,2,768]{2,1,0:T(2,128)S(1)}, f32[2,2,768]{2,1,0:T(2,128)S(1)}, f32[2,2,768,256]{3,2,1,0:T(8,128)}) %tuple.138, (s32[]{:T(128)}, bf16[768,2,256]{2,0,1:T(8,128)(2,1)}, ...), branch_computations={%region_21.21_spmd, %region_22.0_spmd} | conditional | flops 2450529024 | bytes 43456588 | solution.py:29
  325.4 6.2 %multiply_add_fusion.6 = f32[2,2,768,256]{3,2,1,0:T(8,128)} fusion(f32[2,2,768,256]{3,2,1,0:T(8,128)} %get-tuple-element.617, f32[2,768,768,2]{2,1,3,0:T(8,128)S(1)} %get-tuple-element.745, f32[2,2,768]{2,1,0:T(2,128)S(1)} %max.16, pred[768,768]{0,1:T(8,128)(4,1)S(1)} %fusion.78, f32[2,2,768]{2,1,0:T(2,128)S(1)} %get-tuple-element.731, ...), kind=kOutput, calls=%fused_computation.92 | convolution fusion | flops 1221328896 | bytes 17129472 | tf_op jit(solution)/shard_map/while/body/eval_jaxpr/cond/branch_1_fun/hgqk,khd->hgqd/dot_general | solution.py:21
  331.6 12.6 %conditional.12 = ((f32[2,2,768]{2,1,0:T(2,128)S(1)}, f32[2,2,768]{2,1,0:T(2,128)S(1)}, f32[2,2,768,256]{3,2,1,0:T(8,128)})) conditional(s32[]{:T(128)} %convert_element_type.162, (f32[2,2,768]{2,1,0:T(2,128)S(1)}, f32[2,2,768]{2,1,0:T(2,128)S(1)}, f32[2,2,768,256]{3,2,1,0:T(8,128)}) %tuple.135, (s32[]{:T(128)}, bf16[768,2,256]{2,0,1:T(8,128)(2,1)}, ...), branch_computations={%region_13.13_spmd, %region_14.16_spmd} | conditional | flops 2450529024 | bytes 43456588 | solution.py:29
  338.1 6.2 %multiply_add_fusion.2 = f32[2,2,768,256]{3,2,1,0:T(8,128)} fusion(f32[2,2,768,256]{3,2,1,0:T(8,128)} %get-tuple-element.603, f32[2,768,768,2]{2,1,3,0:T(8,128)S(1)} %get-tuple-element.741, f32[2,2,768]{2,1,0:T(2,128)S(1)} %max.14, pred[768,768]{0,1:T(8,128)(4,1)S(1)} %fusion.44, f32[2,2,768]{2,1,0:T(2,128)S(1)} %get-tuple-element.727, ...), kind=kOutput, calls=%fused_computation.50 | convolution fusion | flops 1221328896 | bytes 17129472 | tf_op jit(solution)/shard_map/while/body/eval_jaxpr/cond/branch_1_fun/hgqk,khd->hgqd/dot_general | solution.py:21
  350.4 16.1 %collective-permute-done = bf16[2,768,2,256]{3,1,2,0:T(8,128)(2,1)S(1)} collective-permute-done((bf16[2,768,2,256]{3,1,2,0:T(8,128)(2,1)}, bf16[2,768,2,256]{3,1,2,0:T(8,128)(2,1)S(1)}, u32[]{:S(2)}, u32[]{:S(2)}) %collective-permute-start) | collective-permute-done | bytes 1572896 | tf_op jit(solution)/shard_map/while/body/eval_jaxpr/ppermute | solution.py:67
  367.8 15.6 %collective-permute-done.1 = bf16[2,768,2,256]{3,1,2,0:T(8,128)(2,1)S(1)} collective-permute-done((bf16[2,768,2,256]{3,1,2,0:T(8,128)(2,1)}, bf16[2,768,2,256]{3,1,2,0:T(8,128)(2,1)S(1)}, u32[]{:S(2)}, u32[]{:S(2)}) %collective-permute-start.1) | collective-permute-done | bytes 1572896 | tf_op jit(solution)/shard_map/while/body/eval_jaxpr/ppermute | solution.py:67
  384.6 12.6 %conditional.14 = ((f32[2,2,768]{2,1,0:T(2,128)S(1)}, f32[2,2,768]{2,1,0:T(2,128)S(1)}, f32[2,2,768,256]{3,2,1,0:T(8,128)})) conditional(s32[]{:T(128)} %convert_element_type.164, (f32[2,2,768]{2,1,0:T(2,128)S(1)}, f32[2,2,768]{2,1,0:T(2,128)S(1)}, f32[2,2,768,256]{3,2,1,0:T(8,128)}) %tuple.138, (s32[]{:T(128)}, bf16[768,2,256]{2,0,1:T(8,128)(2,1)}, ...), branch_computations={%region_21.21_spmd, %region_22.0_spmd} | conditional | flops 2450529024 | bytes 43456588 | solution.py:29
  391.0 6.2 %multiply_add_fusion.6 = f32[2,2,768,256]{3,2,1,0:T(8,128)} fusion(f32[2,2,768,256]{3,2,1,0:T(8,128)} %get-tuple-element.617, f32[2,768,768,2]{2,1,3,0:T(8,128)S(1)} %get-tuple-element.745, f32[2,2,768]{2,1,0:T(2,128)S(1)} %max.16, pred[768,768]{0,1:T(8,128)(4,1)S(1)} %fusion.78, f32[2,2,768]{2,1,0:T(2,128)S(1)} %get-tuple-element.731, ...), kind=kOutput, calls=%fused_computation.92 | convolution fusion | flops 1221328896 | bytes 17129472 | tf_op jit(solution)/shard_map/while/body/eval_jaxpr/cond/branch_1_fun/hgqk,khd->hgqd/dot_general | solution.py:21
  397.2 12.6 %conditional.15 = ((f32[2,2,768]{2,1,0:T(2,128)S(1)}, f32[2,2,768]{2,1,0:T(2,128)S(1)}, f32[2,2,768,256]{3,2,1,0:T(8,128)})) conditional(s32[]{:T(128)} %convert_element_type.163, (f32[2,2,768]{2,1,0:T(2,128)S(1)}, f32[2,2,768]{2,1,0:T(2,128)S(1)}, f32[2,2,768,256]{3,2,1,0:T(8,128)}) %get-tuple-element.973, (s32[]{:T(128)}, ...), branch_computations={%region_25.25_spmd, %region_26.0_spmd} | conditional | flops 2450529024 | bytes 43456588 | solution.py:29
  403.6 6.2 %multiply_add_fusion.8 = f32[2,2,768,256]{3,2,1,0:T(8,128)} fusion(f32[2,2,768,256]{3,2,1,0:T(8,128)} %get-tuple-element.624, f32[2,768,768,2]{2,1,3,0:T(8,128)S(1)} %get-tuple-element.747, f32[2,2,768]{2,1,0:T(2,128)S(1)} %max.17, pred[768,768]{0,1:T(8,128)(4,1)S(1)} %fusion.95, f32[2,2,768]{2,1,0:T(2,128)S(1)} %get-tuple-element.733, ...), kind=kOutput, calls=%fused_computation.113 | convolution fusion | flops 1221328896 | bytes 17129472 | tf_op jit(solution)/shard_map/while/body/eval_jaxpr/cond/branch_1_fun/hgqk,khd->hgqd/dot_general | solution.py:21
  417.6 10.2 %convolution_bitcast_fusion = f32[1536,2304]{1,0:T(8,128)} fusion(bf16[1536,256,2,2]{1,0,3,2:T(8,128)(2,1)S(1)} %bitcast.265, bf16[2,2,256,2304]{3,2,1,0:T(8,128)(2,1)S(1)} %bitcast.280), kind=kOutput, calls=%fused_computation.133 | convolution fusion | flops 7247757312 | bytes 22020096 | tf_op jit(solution)/shard_map/ahgqd,hgde->aqe/dot_general | solution.py:74
  427.8 158.8 %reduce-scatter.2.cloned.1.call-done = f32[768,2304]{1,0:T(8,128)} async-done(((f32[1536,2304]{1,0:T(8,128)}), f32[768,2304]{1,0:T(8,128)}) %reduce-scatter.2.cloned.1.call-update) | async-done | bytes 7077904 | tf_op jit(solution)/shard_map/reduce_scatter | solution.py:75
  (157 shorter events, 133.5 us)
Async XLA Ops:
  6.5 90.5 %all-gather.2.cloned.1.call-start = ((), (), s32[]{:S(2)}) async-start(), calls=%async_computation.1 | async-start | bytes 10616832 | tf_op jit(solution)/shard_map/all_gather | solution.py:37
  7.3 579.4 %reduce-scatter.2.cloned.1.call-start = ((), (), s32[]{:S(2)}) async-start(), calls=%async_computation.2 | async-start | bytes 21233664 | tf_op jit(solution)/shard_map/reduce_scatter | solution.py:75
  7.3 6.2 %copy-start.15 = (bf16[2304,2,256]{2,1,0:T(2,128)(2,1)S(1)}, bf16[2304,2,256]{2,1,0:T(2,128)(2,1)}, u32[]{:S(2)}) copy-start(bf16[2304,2,256]{2,1,0:T(2,128)(2,1)} %param.21) | copy-start | bytes 7077892
  13.5 2.3 copy-start.16
  148.3 3.3 copy-start.13
  148.4 3.3 copy-start.17
  148.4 3.3 copy-start.18
  151.6 6.5 %copy-start = (f32[2,768,768,2]{2,1,3,0:T(8,128)}, f32[2,768,768,2]{2,1,3,0:T(8,128)S(1)}, u32[]{:S(2)}) copy-start(f32[2,768,768,2]{2,1,3,0:T(8,128)S(1)} %fusion.137) | copy-start | bytes 28311556
  164.1 9.9 %copy-start.9 = (bf16[768,512]{0,1:T(8,128)(2,1)S(1)}, bf16[768,512]{0,1:T(8,128)(2,1)}, u32[]{:S(2)}) copy-start(bf16[768,512]{0,1:T(8,128)(2,1)} %get-tuple-element.758) | copy-start | bytes 2359300
  164.1 9.9 %copy-start.20 = (bf16[768,512]{0,1:T(8,128)(2,1)S(1)}, bf16[768,512]{0,1:T(8,128)(2,1)}, u32[]{:S(2)}) copy-start(bf16[768,512]{0,1:T(8,128)(2,1)} %get-tuple-element.757) | copy-start | bytes 2359300
  174.0 14.8 %copy-start.14 = (pred[768,768]{0,1:T(8,128)(4,1)S(1)}, pred[768,768]{0,1:T(8,128)(4,1)}, u32[]{:S(2)}) copy-start(pred[768,768]{0,1:T(8,128)(4,1)} %fusion.119) | copy-start | bytes 1769476
  188.8 10.5 %copy-start.21 = (bf16[768,512]{0,1:T(8,128)(2,1)S(1)}, bf16[768,512]{0,1:T(8,128)(2,1)}, u32[]{:S(2)}) copy-start(bf16[768,512]{0,1:T(8,128)(2,1)} %get-tuple-element.757) | copy-start | bytes 2359300
  188.8 19.7 %slice-start = ((s8[9437184]{0:T(1024)(128)(4,1)}), s8[4194304]{0:T(1024)(128)(4,1)S(1)}, s32[]{:S(2)}) async-start(s8[9437184]{0:T(1024)(128)(4,1)} %bitcast.259), calls=%async_computation.3 | async-start | bytes 8388608
  188.8 19.7 %slice-start.1 = ((s8[9437184]{0:T(1024)(128)(4,1)}), s8[4194304]{0:T(1024)(128)(4,1)S(1)}, s32[]{:S(2)}) async-start(s8[9437184]{0:T(1024)(128)(4,1)} %bitcast.259), calls=%async_computation.4 | async-start | bytes 8388608
  199.4 9.1 %slice-start.2 = ((s8[9437184]{0:T(1024)(128)(4,1)}), s8[1048576]{0:T(1024)(128)(4,1)S(1)}, s32[]{:S(2)}) async-start(s8[9437184]{0:T(1024)(128)(4,1)} %bitcast.259), calls=%async_computation.5 | async-start | bytes 2097152
  199.4 9.1 %copy-start.8 = (bf16[768,1024]{0,1:T(8,128)(2,1)S(1)}, bf16[768,1024]{0,1:T(8,128)(2,1)}, u32[]{:S(2)}) copy-start(bf16[768,1024]{0,1:T(8,128)(2,1)} %get-tuple-element.754) | copy-start | bytes 4718596
  199.4 9.1 %copy-start.19 = (bf16[768,512]{0,1:T(8,128)(2,1)S(1)}, bf16[768,512]{0,1:T(8,128)(2,1)}, u32[]{:S(2)}) copy-start(bf16[768,512]{0,1:T(8,128)(2,1)} %get-tuple-element.759) | copy-start | bytes 2359300
  215.4 19.9 %collective-permute-start = (bf16[2,768,2,256]{3,1,2,0:T(8,128)(2,1)}, bf16[2,768,2,256]{3,1,2,0:T(8,128)(2,1)S(1)}, u32[]{:S(2)}, u32[]{:S(2)}) collective-permute-start(bf16[2,768,2,256]{3,1,2,0:T(8,128)(2,1)} %get-tuple-element.931), channel_id=1, source_target_pairs={{0,1},{1,2},{2,3},{3,0},{4,5},{5,6},{6,7},{7,4}} | collective-permute-start | bytes 4718600 | tf_op jit(solution)/shard_map/while/body/eval_jaxpr/ppermute | solution.py:67
  215.5 36.7 %collective-permute-start.1 = (bf16[2,768,2,256]{3,1,2,0:T(8,128)(2,1)}, bf16[2,768,2,256]{3,1,2,0:T(8,128)(2,1)S(1)}, u32[]{:S(2)}, u32[]{:S(2)}) collective-permute-start(bf16[2,768,2,256]{3,1,2,0:T(8,128)(2,1)} %get-tuple-element.932), channel_id=1, source_target_pairs={{0,1},{1,2},{2,3},{3,0},{4,5},{5,6},{6,7},{7,4}} | collective-permute-start | bytes 4718600 | tf_op jit(solution)/shard_map/while/body/eval_jaxpr/ppermute | solution.py:67
  257.5 2.4 copy-start.3
  270.1 2.4 copy-start.4
  281.1 19.8 %collective-permute-start = (bf16[2,768,2,256]{3,1,2,0:T(8,128)(2,1)}, bf16[2,768,2,256]{3,1,2,0:T(8,128)(2,1)S(1)}, u32[]{:S(2)}, u32[]{:S(2)}) collective-permute-start(bf16[2,768,2,256]{3,1,2,0:T(8,128)(2,1)} %get-tuple-element.931), channel_id=1, source_target_pairs={{0,1},{1,2},{2,3},{3,0},{4,5},{5,6},{6,7},{7,4}} | collective-permute-start | bytes 4718600 | tf_op jit(solution)/shard_map/while/body/eval_jaxpr/ppermute | solution.py:67
  281.1 36.7 %collective-permute-start.1 = (bf16[2,768,2,256]{3,1,2,0:T(8,128)(2,1)}, bf16[2,768,2,256]{3,1,2,0:T(8,128)(2,1)S(1)}, u32[]{:S(2)}, u32[]{:S(2)}) collective-permute-start(bf16[2,768,2,256]{3,1,2,0:T(8,128)(2,1)} %get-tuple-element.932), channel_id=1, source_target_pairs={{0,1},{1,2},{2,3},{3,0},{4,5},{5,6},{6,7},{7,4}} | collective-permute-start | bytes 4718600 | tf_op jit(solution)/shard_map/while/body/eval_jaxpr/ppermute | solution.py:67
  323.1 2.4 copy-start.3
  335.7 2.4 copy-start.4
  346.6 19.8 %collective-permute-start = (bf16[2,768,2,256]{3,1,2,0:T(8,128)(2,1)}, bf16[2,768,2,256]{3,1,2,0:T(8,128)(2,1)S(1)}, u32[]{:S(2)}, u32[]{:S(2)}) collective-permute-start(bf16[2,768,2,256]{3,1,2,0:T(8,128)(2,1)} %get-tuple-element.931), channel_id=1, source_target_pairs={{0,1},{1,2},{2,3},{3,0},{4,5},{5,6},{6,7},{7,4}} | collective-permute-start | bytes 4718600 | tf_op jit(solution)/shard_map/while/body/eval_jaxpr/ppermute | solution.py:67
  346.6 36.7 %collective-permute-start.1 = (bf16[2,768,2,256]{3,1,2,0:T(8,128)(2,1)}, bf16[2,768,2,256]{3,1,2,0:T(8,128)(2,1)S(1)}, u32[]{:S(2)}, u32[]{:S(2)}) collective-permute-start(bf16[2,768,2,256]{3,1,2,0:T(8,128)(2,1)} %get-tuple-element.932), channel_id=1, source_target_pairs={{0,1},{1,2},{2,3},{3,0},{4,5},{5,6},{6,7},{7,4}} | collective-permute-start | bytes 4718600 | tf_op jit(solution)/shard_map/while/body/eval_jaxpr/ppermute | solution.py:67
  388.7 2.4 copy-start.3
  401.3 2.4 copy-start.1
  412.4 2.8 copy-start.10
  415.2 2.2 slice-start.3
  415.7 1.9 slice-start.4
  (3 other events, 4.0 us)
Sparse Core Ops, SparseCore 0:
  8.8 88.1 all-gather.1
  427.9 158.6 reduce-scatter.1
where the time goes:
time: 604 us; the launch traced here: 599 us
  waiting for transfers between devices  333 us (55%)
  matrix products  129 us (21%)
  local copies, waits for them, and re-layouts  78.9 us (13%)
  other arithmetic  43.5 us (7%)
  between operations  13.9 us (2%)
    reduce_scatter x1, waiting for transfers between devices, local_attn(): y_rows = lax.psum_scatter(part_sum, 'tp', scatter_dimension=0, tiled=True)  159 us
    ppermute x6, waiting for transfers between devices, ring_free_step(): k_blocks, v_blocks = lax.ppermute((k_blocks, v_blocks), 'sp', next_pairs)  94.8 us
    all_gather x1, waiting for transfers between devices, local_attn(): x_block = lax.all_gather(x_part, 'tp', axis=0, tiled=True)  78.3 us
    dot_general x9, matrix products, block_update(): jnp.einsum('hgqk,khd->hgqd', prob_blk.astype(jnp.bfloat16), v_blk, prefer...  58.4 us
    dot_general x9, matrix products, block_update(): jnp.einsum('qhgd,khd->hgqk', q_blk, k_blk, preferred_element_type=jnp.flo...  33.3 us
    reduce_sum x8, other arithmetic, block_update(): new_sum = row_sum * rescale + jnp.sum(prob_blk, axis=-1)  26.7 us
    unnamed x45, local copies, waits for them, and re-layouts  16.1 us
    while x3, local copies, waits for them, and re-layouts, local_attn(): lax.fori_loop(1, sp_size, ring_free_step, (k_loc, v_loc, states))  15.9 us
  transfers between devices with their start and end apart: 8, of which 8 were waited for; matrix products, arithmetic and copies ran while one was open for 4% of the time, Pallas kernels for 0%

commit v1 on v0

v1 whole, which is shorter than its diff:
```python
import functools

import jax
import jax.numpy as jnp
from jax import lax
from jax.experimental import pallas as pl
from jax.experimental.pallas import tpu as pltpu
from jax.sharding import PartitionSpec as P

MESH = pl.DeviceIdType.MESH
F32 = jnp.float32
BF16 = jnp.bfloat16
NEG_BIG = -1e30
D = 2304
CHUNK = 768
TILE = 256
HEAD = 256
SPAN = 16
EXP_SCALE = 1.4426950408889634 * HEAD**-0.5
X_CHUNKS = ((0, 256), (256, 256), (512, 128), (640, 128))
NX = len(X_CHUNKS)


def nt_dot(a, b):
    return lax.dot_general(a, b, (((1,), (1,)), ((), ())), preferred_element_type=F32)


def kernel(x_ref, wq_ref, wk_ref, wv_ref, wo_ref, y_ref,
           x_buf, w_buf, kv_buf, q_buf, o_own, o_oth, o_rx, wo_own, wo_rx, y_acc, y_bf,
           m_sc, l_sc, acc_sc,
           xs, xr, ws, wr, os, orx, kvs, kvr, loc, ysem):
    tp = lax.axis_index("tp")
    r = lax.axis_index("sp")
    r1 = r + 1 - 2 * (r % 2)
    r2 = (r + 2) % 4
    peer_t = {"tp": 1 - tp, "sp": r}
    peer_x = {"tp": tp, "sp": r2}
    peer_c = {"tp": tp, "sp": r1}

    def block_id(rank, half):
        own = rank + tp * (7 - 2 * rank)
        return own if half == 0 else 7 - own

    def is_low(half):
        return tp == half

    def cond_x_send(half):
        return is_low(half) | (r >= 2)

    def cond_x_recv(half):
        return is_low(half) | (r < 2)

    def cond_c_send(half):
        return is_low(half) | (r % 2 == 1)

    def cond_c_recv(half):
        return is_low(half) | (r % 2 == 0)

    def remote(src, dst, send_sem, recv_sem, peer):
        return pltpu.make_async_remote_copy(src_ref=src, dst_ref=dst, send_sem=send_sem, recv_sem=recv_sem,
                                            device_id=peer, device_id_type=MESH)

    barrier = pltpu.get_barrier_semaphore()
    for peer in (peer_t, peer_x, peer_c):
        pl.semaphore_signal(barrier, inc=1, device_id=peer, device_id_type=MESH)
    pl.semaphore_wait(barrier, 3)

    def x_copy(c):
        row, n = X_CHUNKS[c]
        return remote(x_ref.at[pl.ds(row, n)], x_buf.at[1, pl.ds(row, n)], xs.at[c], xr.at[c], peer_t)

    for c in range(NX):
        x_copy(c).start()

    loads = [
        pltpu.make_async_copy(wk_ref, w_buf.at[pl.ds(0, 2)], loc.at[0]),
        pltpu.make_async_copy(wv_ref, w_buf.at[pl.ds(2, 2)], loc.at[1]),
        pltpu.make_async_copy(x_ref.at[pl.ds(0, 256)], x_buf.at[0, pl.ds(0, 256)], loc.at[2]),
        pltpu.make_async_copy(wq_ref, w_buf.at[pl.ds(4, 4)], loc.at[3]),
        pltpu.make_async_copy(x_ref.at[pl.ds(256, 512)], x_buf.at[0, pl.ds(256, 512)], loc.at[4]),
        pltpu.make_async_copy(wo_ref, wo_own, loc.at[5]),
    ]
    for copy in loads:
        copy.start()

    def kv_slices(half):
        return [(t, 0, TILE) for t in range(3)] if half == 0 else [(row // TILE, row % TILE, n) for row, n in X_CHUNKS]

    def kv_copy(half, c, kind):
        t, row, n = kv_slices(half)[c]
        src_rank = r2 if kind == 2 else r
        part = kv_buf.at[3 * block_id(src_rank, half) + t, :, pl.ds(row, n)]
        slot = (half * 3 + kind) * NX + c
        return remote(part, part, kvs.at[slot], kvr.at[slot], peer_x if kind == 0 else peer_c)

    def kv_recv_wait(half, c, kind):
        t, row, n = kv_slices(half)[c]
        src_rank = (r2, r1, 3 - r)[kind]
        part = kv_buf.at[3 * block_id(src_rank, half) + t, :, pl.ds(row, n)]
        slot = (half * 3 + kind) * NX + c
        remote(part, part, kvs.at[slot], kvr.at[slot], peer_x if kind == 0 else peer_c).wait_recv()

    def kv_send(half, c):
        @pl.when(cond_x_send(half))
        def _():
            kv_copy(half, c, 0).start()

        @pl.when(cond_c_send(half))
        def _():
            kv_copy(half, c, 1).start()

    def kv_forward(half, c):
        @pl.when(cond_x_recv(half))
        def _():
            kv_recv_wait(half, c, 0)
            kv_copy(half, c, 2).start()

    def kv_arrivals(half):
        for c in range(len(kv_slices(half))):
            @pl.when(cond_c_recv(half))
            def _():
                kv_recv_wait(half, c, 1)

            @pl.when(cond_x_recv(half))
            def _():
                kv_recv_wait(half, c, 2)

    def kv_drain(half):
        for c in range(len(kv_slices(half))):
            @pl.when(cond_x_send(half))
            def _():
                kv_copy(half, c, 0).wait_send()

            @pl.when(cond_c_send(half))
            def _():
                kv_copy(half, c, 1).wait_send()

            @pl.when(cond_x_recv(half))
            def _():
                kv_copy(half, c, 2).wait_send()

    def project_kv(half, row, n):
        tile = 3 * block_id(r, half) + row // TILE

        def step(j, _):
            kv_buf[tile, j, pl.ds(row % TILE, n)] = jnp.dot(
                x_buf[half, pl.ds(row, n)], w_buf[j], preferred_element_type=F32).astype(BF16)
            return 0

        lax.fori_loop(0, 4, step, 0)

    def project_q(half, row, n):
        def step(h, _):
            q_buf[half * 6 + (row // TILE) * 2 + h // 2, h % 2, pl.ds(row % TILE, n)] = jnp.dot(
                x_buf[half, pl.ds(row, n)], w_buf[4 + h], preferred_element_type=F32).astype(BF16)
            return 0

        lax.fori_loop(0, 4, step, 0)

    rows_i = lax.broadcasted_iota(jnp.int32, (TILE, TILE), 0)
    cols_i = lax.broadcasted_iota(jnp.int32, (TILE, TILE), 1)

    def attend(half, t, out):
        t_q = 3 * block_id(r, half) + t // 2
        g = t % 2
        q_at = half * 6 + t

        def lanes(p):
            total = p[:, :128]
            for i in range(1, p.shape[1] // 128):
                total = total + p[:, i * 128:(i + 1) * 128]
            return total

        for h in range(2):
            s = jnp.where(cols_i <= rows_i, nt_dot(q_buf[q_at, h], kv_buf[t_q, g]), NEG_BIG)
            m = jnp.max(s, axis=1, keepdims=True)
            p = jnp.exp2((s - m) * EXP_SCALE)
            m_sc[h] = jnp.broadcast_to(m, (TILE, 128))
            l_sc[h] = lanes(p)
            acc_sc[h] = jnp.dot(p.astype(BF16), kv_buf[t_q, 2 + g], preferred_element_type=F32)

        def update(h, tile, count, mask):
            q = q_buf[q_at, h]
            parts = [nt_dot(q, kv_buf[tile + i, g]) for i in range(count)]
            s = parts[0] if count == 1 else jnp.concatenate(parts, axis=1)
            if mask is not None:
                s = jnp.where(mask, s, NEG_BIG)
            m_old = m_sc[h][:, :1]
            m = jnp.maximum(m_old, jnp.max(s, axis=1, keepdims=True))
            p = jnp.exp2((s - m) * EXP_SCALE)
            alpha = jnp.exp2((m_old - m) * EXP_SCALE)
            m_sc[h] = jnp.broadcast_to(m, (TILE, 128))
            l_sc[h] = l_sc[h] * alpha + lanes(p)
            v = kv_buf[tile, 2 + g] if count == 1 else jnp.concatenate(
                [kv_buf[tile + i, 2 + g] for i in range(count)], axis=0)
            acc_sc[h] = acc_sc[h] * alpha + jnp.dot(p.astype(BF16), v, preferred_element_type=F32)

        @pl.when(t_q >= SPAN)
        def _():
            for h in range(2):
                update(h, t_q - SPAN, 1, cols_i > rows_i)

        n = jnp.where(t_q < SPAN - 1, t_q, SPAN - 1)
        low = t_q - n

        def step(i, _):
            for h in range(2):
                update(h, low + 2 * i, 2, None)
            return 0

        lax.fori_loop(0, n // 2, step, 0)

        @pl.when(n % 2 == 1)
        def _():
            for h in range(2):
                update(h, t_q - 1, 1, None)

        for h in range(2):
            total = jnp.sum(l_sc[h], axis=1, keepdims=True)
            out[t, :, h * HEAD:(h + 1) * HEAD] = (acc_sc[h] / total).astype(BF16)

    def o_copy(t):
        return remote(o_oth.at[t], o_rx.at[t], os.at[t], orx.at[t], peer_t)

    def wo_copy(kind):
        src = wo_ref.at[r] if kind == 0 else wo_rx.at[r2] if kind == 3 else wo_rx.at[r]
        dst = wo_rx.at[r2] if kind == 3 else wo_rx.at[r]
        peer = (peer_t, peer_x, peer_c, peer_c)[kind]
        return remote(src, dst, ws.at[kind], wr.at[kind], peer)

    def wo_recv_wait(kind):
        head = (r, r2, r1, 3 - r)[kind]
        remote(wo_rx.at[head], wo_rx.at[head], ws.at[kind], wr.at[kind], peer_t).wait_recv()

    for c in range(3):
        if c == 0:
            loads[0].wait()
            loads[1].wait()
            loads[2].wait()
        if c == 1:
            loads[4].wait()
        project_kv(0, c * TILE, TILE)
        kv_send(0, c)
        if c == 0:
            loads[3].wait()
        project_q(0, c * TILE, TILE)

    def other_rows(c):
        row, n = X_CHUNKS[c]
        x_copy(c).wait_recv()
        project_kv(1, row, n)
        kv_send(1, c)
        project_q(1, row, n)

    kv_forward(0, 0)
    other_rows(0)
    kv_forward(0, 1)
    kv_forward(0, 2)
    kv_arrivals(0)

    @pl.when(tp == 0)
    def _():
        def own(t, _):
            attend(0, t, o_own)
            return 0

        lax.fori_loop(0, 6, own, 0)

    other_rows(1)
    wo_copy(0).start()
    kv_forward(1, 0)
    other_rows(2)
    kv_forward(1, 1)
    other_rows(3)
    kv_forward(1, 2)
    kv_forward(1, 3)
    kv_arrivals(1)

    def other(t, _):
        attend(1, t, o_oth)
        o_copy(t).start()
        return 0

    lax.fori_loop(0, 6, other, 0)

    wo_recv_wait(0)
    wo_copy(1).start()
    wo_copy(2).start()

    @pl.when(tp == 1)
    def _():
        def own(t, _):
            attend(0, t, o_own)
            return 0

        lax.fori_loop(0, 6, own, 0)

    wo_recv_wait(1)
    wo_copy(3).start()
    loads[5].wait()

    def own_out(i, _):
        for j in range(3):
            cols = slice(j * CHUNK, (j + 1) * CHUNK)
            w = wo_own[:, :, cols].reshape(4 * HEAD, CHUNK)
            o = jnp.concatenate([o_own[2 * i], o_own[2 * i + 1]], axis=1)
            y_acc[i, :, cols] = jnp.dot(o, w, preferred_element_type=F32)
        return 0

    lax.fori_loop(0, 3, own_out, 0)
    wo_recv_wait(2)
    wo_recv_wait(3)

    def y_copy(i):
        return pltpu.make_async_copy(y_bf.at[pl.ds(i * TILE, TILE)], y_ref.at[pl.ds(i * TILE, TILE)], ysem.at[i])

    for i in range(3):
        for g in range(2):
            o_copy(2 * i + g).wait_recv()
            for j in range(3):
                cols = slice(j * CHUNK, (j + 1) * CHUNK)
                w = wo_rx[2 * g:2 * g + 2, :, cols].reshape(2 * HEAD, CHUNK)
                total = y_acc[i, :, cols] + jnp.dot(o_rx[2 * i + g], w, preferred_element_type=F32)
                if g == 0:
                    y_acc[i, :, cols] = total
                else:
                    y_bf[i * TILE:(i + 1) * TILE, cols] = total.astype(BF16)
        y_copy(i).start()

    for c in range(NX):
        x_copy(c).wait_send()
    kv_drain(0)
    kv_drain(1)
    for kind in range(4):
        wo_copy(kind).wait_send()
    for t in range(6):
        o_copy(t).wait_send()
    for i in range(3):
        y_copy(i).wait()


def solution(mesh):
    def local_attn(x, wq, wk, wv, wo):
        wq_t = wq.transpose(1, 0, 2)
        wk_t = wk.transpose(1, 0, 2)
        wv_t = wv.transpose(1, 0, 2)
        any_spec = pl.BlockSpec(memory_space=pl.ANY)
        return pl.pallas_call(
            kernel,
            out_shape=jax.ShapeDtypeStruct((CHUNK, D), BF16),
            in_specs=[any_spec] * 5,
            out_specs=any_spec,
            scratch_shapes=[
                pltpu.VMEM((2, CHUNK, D), BF16),
                pltpu.VMEM((8, D, HEAD), BF16),
                pltpu.VMEM((24, 4, TILE, HEAD), BF16),
                pltpu.VMEM((12, 2, TILE, HEAD), BF16),
                pltpu.VMEM((6, TILE, 2 * HEAD), BF16),
                pltpu.VMEM((6, TILE, 2 * HEAD), BF16),
                pltpu.VMEM((6, TILE, 2 * HEAD), BF16),
                pltpu.VMEM((4, HEAD, D), BF16),
                pltpu.VMEM((4, HEAD, D), BF16),
                pltpu.VMEM((3, TILE, D), F32),
                pltpu.VMEM((CHUNK, D), BF16),
                pltpu.VMEM((2, TILE, 128), F32),
                pltpu.VMEM((2, TILE, 128), F32),
                pltpu.VMEM((2, TILE, HEAD), F32),
                pltpu.SemaphoreType.DMA((NX,)),
                pltpu.SemaphoreType.DMA((NX,)),
                pltpu.SemaphoreType.DMA((4,)),
                pltpu.SemaphoreType.DMA((4,)),
                pltpu.SemaphoreType.DMA((6,)),
                pltpu.SemaphoreType.DMA((6,)),
                pltpu.SemaphoreType.DMA((6 * NX,)),
                pltpu.SemaphoreType.DMA((6 * NX,)),
                pltpu.SemaphoreType.DMA((6,)),
                pltpu.SemaphoreType.DMA((3,)),
            ],
            compiler_params=pltpu.CompilerParams(collective_id=0, has_side_effects=True, vmem_limit_bytes=66 * 1024 * 1024 - 2 * 1024 * 1024 - 65536),
            name="attn_block",
        )(x, wq_t, wk_t, wv_t, wo)

    return jax.shard_map(local_attn, mesh=mesh, in_specs=(P(("dp", "sp", "tp"), None), P(None, "tp", None), P(None, "tp", None), P(None, "tp", None), P("tp", None, None)), out_specs=P(("dp", "sp", "tp"), None), check_vma=False)
```

time: 604 us -> 205 us (0.34)
  waiting for transfers between devices: 333 us -> 0 us
  Pallas kernels: 0 us -> 192 us
  matrix products: 129 us -> 0 us
  local copies, waits for them, and re-layouts: 78.9 us -> 12.2 us
  other arithmetic: 43.5 us -> 0 us
  between operations: 13.9 us -> 0.01 us
    pallas_call x0 -> x1, Pallas kernels: none -> 192 us  [local_attn(): pl.pallas_call(kernel, out_shape=jax.ShapeDtypeStruct((CHUNK, D), BF16),...]
    reduce_scatter x1 -> x0, waiting for transfers between devices: 159 us -> none  [local_attn(): y_rows = lax.psum_scatter(part_sum, 'tp', scatter_dimension=0, tiled=True)]
    dot_general x22 -> x0, matrix products: 129 us -> none  [the longest x9 58.4 us: block_update(): jnp.einsum('hgqk,khd->hgqd', prob_blk.astype(jnp.bfloat16), v_blk, prefer...]
    ppermute x6 -> x0, waiting for transfers between devices: 94.8 us -> none  [ring_free_step(): k_blocks, v_blocks = lax.ppermute((k_blocks, v_blocks), 'sp', next_pairs)]
    all_gather x1 -> x0, waiting for transfers between devices: 78.3 us -> none  [local_attn(): x_block = lax.all_gather(x_part, 'tp', axis=0, tiled=True)]
    reduce_sum x8 -> x0, other arithmetic: 26.7 us -> none  [block_update(): new_sum = row_sum * rescale + jnp.sum(prob_blk, axis=-1)]
    while x9 -> x0, local copies, waits for them, and re-layouts: 23 us -> none  [the longest x3 15.9 us: local_attn(): lax.fori_loop(1, sp_size, ring_free_step, (k_loc, v_loc, states))]
    squeeze x9 -> x0, local copies, waits for them, and re-layouts: 19 us -> none  [the longest x3 11.2 us: absorb(): q_loc[q_half]]
  transfers between devices with their start and end apart: 8 -> 0, of which waited for: 8 -> 0; matrix products, arithmetic and copies ran while one was open for 4% -> 0% of each run, Pallas kernels for 0% -> 0%
where the time goes in v1:
time: 205 us; the launch traced here: 204 us
  Pallas kernels  192 us (94%)
  local copies, waits for them, and re-layouts  12.2 us (6%)
    pallas_call x1, Pallas kernels, local_attn(): pl.pallas_call(kernel, out_shape=jax.ShapeDtypeStruct((CHUNK, D), BF16),...  192 us
    unnamed x6, local copies, waits for them, and re-layouts  9.24 us

profile of v1, /device:TPU:2, one launch (start us, length us, event | category | flops | bytes accessed | tf_op | source)
XLA Modules:
  0.0 204.5 jit_solution(12461992562533318880)
XLA Ops:
  0.0 0.0 copy-start
  0.0 0.0 copy-start.1
  0.0 5.2 %copy.12 = bf16[2304,4,256]{2,0,1:T(8,128)(2,1)} copy(bf16[2304,4,256]{2,1,0:T(4,128)(2,1)} %param.6) | data formatting | bytes 9437184 | tf_op args[1]
  5.2 0.0 copy-done
  5.2 0.0 copy-done.1
  5.2 2.9 %copy_bitcast_fusion.1 = (bf16[2,2304,256]{2,1,0:T(8,128)(2,1)}, bf16[2,2304,256]{2,1,0:T(8,128)(2,1)}) fusion(bf16[2304,2,256]{2,1,0:T(2,128)(2,1)S(1)} %copy-done, bf16[2304,2,256]{2,1,0:T(2,128)(2,1)S(1)} %copy-done.1), kind=kLoop, calls=%fused_computation.1 | loop fusion | bytes 9437184 | tf_op jit(solution)/shard_map/transpose | solution.py:346
  8.1 192.3 %attn_block.1 = bf16[768,2304]{1,0:T(8,128)(2,1)} custom-call(bf16[768,2304]{1,0:T(8,128)(2,1)} %x_ref.1, bf16[4,2304,256]{2,1,0:T(8,128)(2,1)} %bitcast.7, bf16[2,2304,256]{2,1,0:T(8,128)(2,1)} %get-tuple-element.6.wk_ref, bf16[2,2304,256]{2,1,0:T(8,128)(2,1)} %get-tuple-element.5.wv_ref, bf16[4,256,2304]{2,1,0:T(8,128)(2,1)} %wo_ref.1), custom_call_target="tpu_custom_call" | custom-call | tf_op jit(solution)/shard_map/attn_block/pallas_call | solution.py:348
  200.4 4.0 %copy.14 = bf16[768,2304]{1,0:T(8,128)(2,1)} copy(bf16[768,2304]{1,0:T(8,128)(2,1)} %attn_block.1) | data formatting | bytes 7077888
Async XLA Ops:
  0.0 5.2 %copy-start = (bf16[2304,2,256]{2,1,0:T(2,128)(2,1)S(1)}, bf16[2304,2,256]{2,1,0:T(2,128)(2,1)}, u32[]{:S(2)}) copy-start(bf16[2304,2,256]{2,1,0:T(2,128)(2,1)} %param.8) | copy-start | bytes 7077892
  0.0 5.2 %copy-start.1 = (bf16[2304,2,256]{2,1,0:T(2,128)(2,1)S(1)}, bf16[2304,2,256]{2,1,0:T(2,128)(2,1)}, u32[]{:S(2)}) copy-start(bf16[2304,2,256]{2,1,0:T(2,128)(2,1)} %param.7) | copy-start | bytes 7077892

commit v2 on v1

--- a/solution.py
+++ b/solution.py
@@ -27,7 +27,7 @@
 
 def kernel(x_ref, wq_ref, wk_ref, wv_ref, wo_ref, y_ref,
            x_buf, w_buf, kv_buf, q_buf, o_own, o_oth, o_rx, wo_own, wo_rx, y_acc, y_bf,
-           m_sc, l_sc, acc_sc,
+           m_sc, l_sc, acc_sc, s0_sc, sa_sc, sb_sc,
            xs, xr, ws, wr, os, orx, kvs, kvr, loc, ysem):
     tp = lax.axis_index("tp")
     r = lax.axis_index("sp")
@@ -160,60 +160,75 @@
     rows_i = lax.broadcasted_iota(jnp.int32, (TILE, TILE), 0)
     cols_i = lax.broadcasted_iota(jnp.int32, (TILE, TILE), 1)
 
+    gap_i = cols_i - rows_i
+
     def attend(half, t, out):
         t_q = 3 * block_id(r, half) + t // 2
         g = t % 2
         q_at = half * 6 + t
-
-        def lanes(p):
-            total = p[:, :128]
-            for i in range(1, p.shape[1] // 128):
-                total = total + p[:, i * 128:(i + 1) * 128]
-            return total
-
-        for h in range(2):
-            s = jnp.where(cols_i <= rows_i, nt_dot(q_buf[q_at, h], kv_buf[t_q, g]), NEG_BIG)
-            m = jnp.max(s, axis=1, keepdims=True)
-            p = jnp.exp2((s - m) * EXP_SCALE)
-            m_sc[h] = jnp.broadcast_to(m, (TILE, 128))
-            l_sc[h] = lanes(p)
-            acc_sc[h] = jnp.dot(p.astype(BF16), kv_buf[t_q, 2 + g], preferred_element_type=F32)
-
-        def update(h, tile, count, mask):
-            q = q_buf[q_at, h]
-            parts = [nt_dot(q, kv_buf[tile + i, g]) for i in range(count)]
-            s = parts[0] if count == 1 else jnp.concatenate(parts, axis=1)
-            if mask is not None:
-                s = jnp.where(mask, s, NEG_BIG)
-            m_old = m_sc[h][:, :1]
-            m = jnp.maximum(m_old, jnp.max(s, axis=1, keepdims=True))
-            p = jnp.exp2((s - m) * EXP_SCALE)
-            alpha = jnp.exp2((m_old - m) * EXP_SCALE)
-            m_sc[h] = jnp.broadcast_to(m, (TILE, 128))
-            l_sc[h] = l_sc[h] * alpha + lanes(p)
-            v = kv_buf[tile, 2 + g] if count == 1 else jnp.concatenate(
-                [kv_buf[tile + i, 2 + g] for i in range(count)], axis=0)
-            acc_sc[h] = acc_sc[h] * alpha + jnp.dot(p.astype(BF16), v, preferred_element_type=F32)
-
-        @pl.when(t_q >= SPAN)
+        far = t_q >= SPAN
+        n_full = jnp.where(t_q < SPAN - 1, t_q, SPAN - 1)
+        low = t_q - n_full
+        take = jnp.where(far, 1, jnp.where(t_q == 0, 0, 2 - t_q % 2))
+        pairs = (n_full - take) // 2
+        tile_b = jnp.where(far, t_q - SPAN, jnp.where(take == 2, t_q - 2, t_q))
+        tile_c = jnp.where(take > 0, t_q - 1, t_q)
+        gap_b = jnp.where(far, 0, jnp.where(take == 2, -TILE, TILE))
+        gap_c = jnp.where(take > 0, -TILE, TILE)
+
+        def pair_tiles(i):
+            start = low + 2 * jnp.where(i < pairs, i, 0)
+            return (start, start + 1)
+
+        def scores(dst, tiles):
+            for h in range(2):
+                q = q_buf[q_at, h]
+                for i, tile in enumerate(tiles):
+                    dst[h, :, i * TILE:(i + 1) * TILE] = nt_dot(q, kv_buf[tile, g])
+
+        def absorb(src, tiles, first):
+            wide = 2 * len(tiles)
+            for h in range(2):
+                s = src[h]
+                if first:
+                    s = jnp.concatenate([
+                        jnp.where(gap_i <= 0, s[:, :TILE], NEG_BIG),
+                        jnp.where(gap_i > gap_b, s[:, TILE:2 * TILE], NEG_BIG),
+                        jnp.where(gap_i > gap_c, s[:, 2 * TILE:], NEG_BIG)], axis=1)
+                top = jnp.broadcast_to(jnp.max(s, axis=1, keepdims=True), (TILE, 128))
+                m = top if first else jnp.maximum(m_sc[h], top)
+                p = jnp.exp2((s - jnp.concatenate([m] * wide, axis=1)) * EXP_SCALE)
+                total = p[:, :128]
+                for i in range(1, wide):
+                    total = total + p[:, i * 128:(i + 1) * 128]
+                v = jnp.concatenate([kv_buf[tile, 2 + g] for tile in tiles], axis=0)
+                o = jnp.dot(p.astype(BF16), v, preferred_element_type=F32)
+                if first:
+                    l_sc[h] = total
+                    acc_sc[h] = o
+                else:
+                    alpha = jnp.exp2((m_sc[h] - m) * EXP_SCALE)
+                    l_sc[h] = l_sc[h] * alpha + total
+                    acc_sc[h] = acc_sc[h] * jnp.concatenate([alpha, alpha], axis=1) + o
+                m_sc[h] = m
+
+        first_tiles = (t_q, tile_b, tile_c)
+        scores(s0_sc, first_tiles)
+        scores(sa_sc, pair_tiles(0))
+        absorb(s0_sc, first_tiles, True)
+
+        def step(j, _):
+            scores(sb_sc, pair_tiles(2 * j + 1))
+            absorb(sa_sc, pair_tiles(2 * j), False)
+            scores(sa_sc, pair_tiles(2 * j + 2))
+            absorb(sb_sc, pair_tiles(2 * j + 1), False)
+            return 0
+
+        lax.fori_loop(0, pairs // 2, step, 0)
+
+        @pl.when(pairs % 2 == 1)
         def _():
-            for h in range(2):
-                update(h, t_q - SPAN, 1, cols_i > rows_i)
-
-        n = jnp.where(t_q < SPAN - 1, t_q, SPAN - 1)
-        low = t_q - n
-
-        def step(i, _):
-            for h in range(2):
-                update(h, low + 2 * i, 2, None)
-            return 0
-
-        lax.fori_loop(0, n // 2, step, 0)
-
-        @pl.when(n % 2 == 1)
-        def _():
-            for h in range(2):
-                update(h, t_q - 1, 1, None)
+            absorb(sa_sc, pair_tiles(pairs - 1), False)
 
         for h in range(2):
             total = jnp.sum(l_sc[h], axis=1, keepdims=True)
@@ -365,6 +380,9 @@
                 pltpu.VMEM((2, TILE, 128), F32),
                 pltpu.VMEM((2, TILE, 128), F32),
                 pltpu.VMEM((2, TILE, HEAD), F32),
+                pltpu.VMEM((2, TILE, 3 * TILE), F32),
+                pltpu.VMEM((2, TILE, 2 * TILE), F32),
+                pltpu.VMEM((2, TILE, 2 * TILE), F32),
                 pltpu.SemaphoreType.DMA((NX,)),
                 pltpu.SemaphoreType.DMA((NX,)),
                 pltpu.SemaphoreType.DMA((4,)),

time: 205 us -> 164 us (0.80)
  Pallas kernels: 192 us -> 151 us
    pallas_call x1, Pallas kernels: 192 us -> 151 us  [local_attn(): pl.pallas_call(kernel, out_shape=jax.ShapeDtypeStruct((CHUNK, D), BF16),...]
where the time goes in v2:
time: 164 us; the launch traced here: 163 us
  Pallas kernels  151 us (92%)
  local copies, waits for them, and re-layouts  12.2 us (7%)
    pallas_call x1, Pallas kernels, local_attn(): pl.pallas_call(kernel, out_shape=jax.ShapeDtypeStruct((CHUNK, D), BF16),...  151 us
    unnamed x6, local copies, waits for them, and re-layouts  9.24 us

profile of v2, /device:TPU:2, one launch (start us, length us, event | category | flops | bytes accessed | tf_op | source)
XLA Modules:
  0.0 163.4 jit_solution(457070397771336060)
XLA Ops:
  0.0 0.0 copy-start
  0.0 0.0 copy-start.1
  0.0 5.2 %copy.12 = bf16[2304,4,256]{2,0,1:T(8,128)(2,1)} copy(bf16[2304,4,256]{2,1,0:T(4,128)(2,1)} %param.6) | data formatting | bytes 9437184 | tf_op args[1]
  5.2 0.0 copy-done
  5.2 0.0 copy-done.1
  5.2 2.9 %copy_bitcast_fusion.1 = (bf16[2,2304,256]{2,1,0:T(8,128)(2,1)}, bf16[2,2304,256]{2,1,0:T(8,128)(2,1)}) fusion(bf16[2304,2,256]{2,1,0:T(2,128)(2,1)S(1)} %copy-done, bf16[2304,2,256]{2,1,0:T(2,128)(2,1)S(1)} %copy-done.1), kind=kLoop, calls=%fused_computation.1 | loop fusion | bytes 9437184 | tf_op jit(solution)/shard_map/transpose | solution.py:361
  8.1 151.3 %attn_block.1 = bf16[768,2304]{1,0:T(8,128)(2,1)} custom-call(bf16[768,2304]{1,0:T(8,128)(2,1)} %x_ref.1, bf16[4,2304,256]{2,1,0:T(8,128)(2,1)} %bitcast.7, bf16[2,2304,256]{2,1,0:T(8,128)(2,1)} %get-tuple-element.6.wk_ref, bf16[2,2304,256]{2,1,0:T(8,128)(2,1)} %get-tuple-element.5.wv_ref, bf16[4,256,2304]{2,1,0:T(8,128)(2,1)} %wo_ref.1), custom_call_target="tpu_custom_call" | custom-call | tf_op jit(solution)/shard_map/attn_block/pallas_call | solution.py:363
  159.4 4.0 %copy.14 = bf16[768,2304]{1,0:T(8,128)(2,1)} copy(bf16[768,2304]{1,0:T(8,128)(2,1)} %attn_block.1) | data formatting | bytes 7077888
Async XLA Ops:
  0.0 5.2 %copy-start = (bf16[2304,2,256]{2,1,0:T(2,128)(2,1)S(1)}, bf16[2304,2,256]{2,1,0:T(2,128)(2,1)}, u32[]{:S(2)}) copy-start(bf16[2304,2,256]{2,1,0:T(2,128)(2,1)} %param.8) | copy-start | bytes 7077892
  0.0 5.2 %copy-start.1 = (bf16[2304,2,256]{2,1,0:T(2,128)(2,1)S(1)}, bf16[2304,2,256]{2,1,0:T(2,128)(2,1)}, u32[]{:S(2)}) copy-start(bf16[2304,2,256]{2,1,0:T(2,128)(2,1)} %param.7) | copy-start | bytes 7077892

commit v3 on v2

--- a/solution.py
+++ b/solution.py
@@ -17,8 +17,9 @@
 HEAD = 256
 SPAN = 16
 EXP_SCALE = 1.4426950408889634 * HEAD**-0.5
-X_CHUNKS = ((0, 256), (256, 256), (512, 128), (640, 128))
+X_CHUNKS = ((0, 256), (256, 256), (512, 192), (704, 64))
 NX = len(X_CHUNKS)
+VMEM_LIMIT = 59 * 1024 * 1024
 
 
 def nt_dot(a, b):
@@ -26,9 +27,9 @@
 
 
 def kernel(x_ref, wq_ref, wk_ref, wv_ref, wo_ref, y_ref,
-           x_buf, w_buf, kv_buf, q_buf, o_own, o_oth, o_rx, wo_own, wo_rx, y_acc, y_bf,
+           x_buf, w_buf, kv_buf, q_buf, o_own, o_oth, o_rx, wo_own, wo_rx, y_acc,
            m_sc, l_sc, acc_sc, s0_sc, sa_sc, sb_sc,
-           xs, xr, ws, wr, os, orx, kvs, kvr, loc, ysem):
+           xs, xr, ws, wr, os, orx, kvs, kvr, loc):
     tp = lax.axis_index("tp")
     r = lax.axis_index("sp")
     r1 = r + 1 - 2 * (r % 2)
@@ -294,13 +295,16 @@
     def other(t, _):
         attend(1, t, o_oth)
         o_copy(t).start()
+
+        @pl.when(t == 3)
+        def _():
+            wo_recv_wait(0)
+            wo_copy(1).start()
+            wo_copy(2).start()
+
         return 0
 
     lax.fori_loop(0, 6, other, 0)
-
-    wo_recv_wait(0)
-    wo_copy(1).start()
-    wo_copy(2).start()
 
     @pl.when(tp == 1)
     def _():
@@ -325,9 +329,6 @@
     lax.fori_loop(0, 3, own_out, 0)
     wo_recv_wait(2)
     wo_recv_wait(3)
-
-    def y_copy(i):
-        return pltpu.make_async_copy(y_bf.at[pl.ds(i * TILE, TILE)], y_ref.at[pl.ds(i * TILE, TILE)], ysem.at[i])
 
     for i in range(3):
         for g in range(2):
@@ -339,8 +340,7 @@
                 if g == 0:
                     y_acc[i, :, cols] = total
                 else:
-                    y_bf[i * TILE:(i + 1) * TILE, cols] = total.astype(BF16)
-        y_copy(i).start()
+                    y_ref[i * TILE:(i + 1) * TILE, cols] = total.astype(BF16)
 
     for c in range(NX):
         x_copy(c).wait_send()
@@ -350,8 +350,6 @@
         wo_copy(kind).wait_send()
     for t in range(6):
         o_copy(t).wait_send()
-    for i in range(3):
-        y_copy(i).wait()
 
 
 def solution(mesh):
@@ -362,9 +360,9 @@
         any_spec = pl.BlockSpec(memory_space=pl.ANY)
         return pl.pallas_call(
             kernel,
-            out_shape=jax.ShapeDtypeStruct((CHUNK, D), BF16),
+            out_shape=pltpu.VMEM((CHUNK, D), BF16),
             in_specs=[any_spec] * 5,
-            out_specs=any_spec,
+            out_specs=pl.BlockSpec(memory_space=pltpu.VMEM),
             scratch_shapes=[
                 pltpu.VMEM((2, CHUNK, D), BF16),
                 pltpu.VMEM((8, D, HEAD), BF16),
@@ -376,7 +374,6 @@
                 pltpu.VMEM((4, HEAD, D), BF16),
                 pltpu.VMEM((4, HEAD, D), BF16),
                 pltpu.VMEM((3, TILE, D), F32),
-                pltpu.VMEM((CHUNK, D), BF16),
                 pltpu.VMEM((2, TILE, 128), F32),
                 pltpu.VMEM((2, TILE, 128), F32),
                 pltpu.VMEM((2, TILE, HEAD), F32),
@@ -392,9 +389,8 @@
                 pltpu.SemaphoreType.DMA((6 * NX,)),
                 pltpu.SemaphoreType.DMA((6 * NX,)),
                 pltpu.SemaphoreType.DMA((6,)),
-                pltpu.SemaphoreType.DMA((3,)),
             ],
-            compiler_params=pltpu.CompilerParams(collective_id=0, has_side_effects=True, vmem_limit_bytes=66 * 1024 * 1024 - 2 * 1024 * 1024 - 65536),
+            compiler_params=pltpu.CompilerParams(collective_id=0, has_side_effects=True, vmem_limit_bytes=VMEM_LIMIT),
             name="attn_block",
         )(x, wq_t, wk_t, wv_t, wo)
 

time: 164 us -> 156 us (0.951)
  the two profiles are of different devices: /device:TPU:2 before, /device:TPU:6 now
where the time goes in v3:
time: 156 us
  Pallas kernels  146 us (94%)
  local copies, waits for them, and re-layouts  9.9 us (6%)
    pallas_call x1, Pallas kernels, local_attn(): pl.pallas_call(kernel, out_shape=pltpu.VMEM((CHUNK, D), BF16), in_specs=[...  146 us
    unnamed x6, local copies, waits for them, and re-layouts  7.01 us

profile of v3, /device:TPU:6, one launch (start us, length us, event | category | flops | bytes accessed | tf_op | source)
XLA Modules:
  0.0 156.1 jit_solution(7460109227728997618)
XLA Ops:
  0.0 0.0 copy-start
  0.0 0.0 copy-start.1
  0.0 5.2 %copy.12 = bf16[2304,4,256]{2,0,1:T(8,128)(2,1)} copy(bf16[2304,4,256]{2,1,0:T(4,128)(2,1)} %param.6) | data formatting | bytes 9437184 | tf_op args[1]
  5.2 0.0 copy-done
  5.2 0.0 copy-done.1
  5.2 2.9 %copy_bitcast_fusion.1 = (bf16[2,2304,256]{2,1,0:T(8,128)(2,1)}, bf16[2,2304,256]{2,1,0:T(8,128)(2,1)}) fusion(bf16[2304,2,256]{2,1,0:T(2,128)(2,1)S(1)} %copy-done, bf16[2304,2,256]{2,1,0:T(2,128)(2,1)S(1)} %copy-done.1), kind=kLoop, calls=%fused_computation.1 | loop fusion | bytes 9437184 | tf_op jit(solution)/shard_map/transpose | solution.py:359
  8.1 146.1 %attn_block.1 = bf16[768,2304]{1,0:T(8,128)(2,1)S(1)} custom-call(bf16[768,2304]{1,0:T(8,128)(2,1)} %x_ref.1, bf16[4,2304,256]{2,1,0:T(8,128)(2,1)} %bitcast.7, bf16[2,2304,256]{2,1,0:T(8,128)(2,1)} %get-tuple-element.6.wk_ref, bf16[2,2304,256]{2,1,0:T(8,128)(2,1)} %get-tuple-element.5.wv_ref, bf16[4,256,2304]{2,1,0:T(8,128)(2,1)} %wo_ref.1), custom_call_target="tpu_custom_call" | custom-call | tf_op jit(solution)/shard_map/attn_block/pallas_call | solution.py:361
  154.3 1.8 %copy.14 = bf16[768,2304]{1,0:T(8,128)(2,1)} copy(bf16[768,2304]{1,0:T(8,128)(2,1)S(1)} %attn_block.1) | data formatting | bytes 7077888
Async XLA Ops:
  0.0 5.2 %copy-start = (bf16[2304,2,256]{2,1,0:T(2,128)(2,1)S(1)}, bf16[2304,2,256]{2,1,0:T(2,128)(2,1)}, u32[]{:S(2)}) copy-start(bf16[2304,2,256]{2,1,0:T(2,128)(2,1)} %param.8) | copy-start | bytes 7077892
  0.0 5.2 %copy-start.1 = (bf16[2304,2,256]{2,1,0:T(2,128)(2,1)S(1)}, bf16[2304,2,256]{2,1,0:T(2,128)(2,1)}, u32[]{:S(2)}) copy-start(bf16[2304,2,256]{2,1,0:T(2,128)(2,1)} %param.7) | copy-start | bytes 7077892

commit v4 on v3

--- a/solution.py
+++ b/solution.py
@@ -18,6 +18,7 @@
 SPAN = 16
 EXP_SCALE = 1.4426950408889634 * HEAD**-0.5
 X_CHUNKS = ((0, 256), (256, 256), (512, 192), (704, 64))
+HEAD_ROWS = 80
 NX = len(X_CHUNKS)
 VMEM_LIMIT = 59 * 1024 * 1024
 
@@ -26,7 +27,7 @@
     return lax.dot_general(a, b, (((1,), (1,)), ((), ())), preferred_element_type=F32)
 
 
-def kernel(x_ref, wq_ref, wk_ref, wv_ref, wo_ref, y_ref,
+def kernel(x_ref, x_head_ref, wq_ref, wk_ref, wv_ref, wo_ref, y_ref,
            x_buf, w_buf, kv_buf, q_buf, o_own, o_oth, o_rx, wo_own, wo_rx, y_acc,
            m_sc, l_sc, acc_sc, s0_sc, sa_sc, sb_sc,
            xs, xr, ws, wr, os, orx, kvs, kvr, loc):
@@ -68,6 +69,8 @@
 
     def x_copy(c):
         row, n = X_CHUNKS[c]
+        if c == 0:
+            row, n = row + HEAD_ROWS, n - HEAD_ROWS
         return remote(x_ref.at[pl.ds(row, n)], x_buf.at[1, pl.ds(row, n)], xs.at[c], xr.at[c], peer_t)
 
     for c in range(NX):
@@ -80,6 +83,7 @@
         pltpu.make_async_copy(wq_ref, w_buf.at[pl.ds(4, 4)], loc.at[3]),
         pltpu.make_async_copy(x_ref.at[pl.ds(256, 512)], x_buf.at[0, pl.ds(256, 512)], loc.at[4]),
         pltpu.make_async_copy(wo_ref, wo_own, loc.at[5]),
+        pltpu.make_async_copy(x_head_ref, x_buf.at[1, pl.ds(0, HEAD_ROWS)], loc.at[6]),
     ]
     for copy in loads:
         copy.start()
@@ -263,6 +267,8 @@
 
     def other_rows(c):
         row, n = X_CHUNKS[c]
+        if c == 0:
+            loads[6].wait()
         x_copy(c).wait_recv()
         project_kv(1, row, n)
         kv_send(1, c)
@@ -296,7 +302,7 @@
         attend(1, t, o_oth)
         o_copy(t).start()
 
-        @pl.when(t == 3)
+        @pl.when(t == 3 + 2 * tp)
         def _():
             wo_recv_wait(0)
             wo_copy(1).start()
@@ -354,6 +360,7 @@
 
 def solution(mesh):
     def local_attn(x, wq, wk, wv, wo):
+        x_head = lax.ppermute(x[:HEAD_ROWS], "tp", ((0, 1), (1, 0)))
         wq_t = wq.transpose(1, 0, 2)
         wk_t = wk.transpose(1, 0, 2)
         wv_t = wv.transpose(1, 0, 2)
@@ -361,7 +368,7 @@
         return pl.pallas_call(
             kernel,
             out_shape=pltpu.VMEM((CHUNK, D), BF16),
-            in_specs=[any_spec] * 5,
+            in_specs=[any_spec, pl.BlockSpec(memory_space=pltpu.HBM)] + [any_spec] * 4,
             out_specs=pl.BlockSpec(memory_space=pltpu.VMEM),
             scratch_shapes=[
                 pltpu.VMEM((2, CHUNK, D), BF16),
@@ -388,10 +395,10 @@
                 pltpu.SemaphoreType.DMA((6,)),
                 pltpu.SemaphoreType.DMA((6 * NX,)),
                 pltpu.SemaphoreType.DMA((6 * NX,)),
-                pltpu.SemaphoreType.DMA((6,)),
+                pltpu.SemaphoreType.DMA((7,)),
             ],
             compiler_params=pltpu.CompilerParams(collective_id=0, has_side_effects=True, vmem_limit_bytes=VMEM_LIMIT),
             name="attn_block",
-        )(x, wq_t, wk_t, wv_t, wo)
+        )(x, x_head, wq_t, wk_t, wv_t, wo)
 
     return jax.shard_map(local_attn, mesh=mesh, in_specs=(P(("dp", "sp", "tp"), None), P(None, "tp", None), P(None, "tp", None), P(None, "tp", None), P("tp", None, None)), out_specs=P(("dp", "sp", "tp"), None), check_vma=False)

time: 156 us -> 151 us (0.968)
  the two profiles are of different devices: /device:TPU:6 before, /device:TPU:2 now
where the time goes in v4:
time: 151 us
  Pallas kernels  137 us (91%)
  local copies, waits for them, and re-layouts  11.6 us (8%)
  starting transfers between devices  1.54 us (1%)
    pallas_call x1, Pallas kernels, local_attn(): pl.pallas_call(kernel, out_shape=pltpu.VMEM((CHUNK, D), BF16), in_specs=[...  137 us
    unnamed x8, local copies, waits for them, and re-layouts  5.28 us
    transpose x1, local copies, waits for them, and re-layouts, local_attn(): wv_t = wv.transpose(1, 0, 2)  5.19 us
  transfers between devices with their start and end apart: 1, of which 1 were waited for; matrix products, arithmetic and copies ran while one was open for 5% of the time, Pallas kernels for 0%

profile of v4, /device:TPU:2, one launch (start us, length us, event | category | flops | bytes accessed | tf_op | source)
XLA Modules:
  0.0 150.8 jit_solution(2462399688724812190)
XLA Ops:
  0.0 0.0 slice-start
  0.0 1.2 slice.3
  1.2 0.0 slice-start.1
  1.2 1.5 %collective-permute-start = (bf16[80,2304]{1,0:T(8,128)(2,1)S(1)}, bf16[80,2304]{1,0:T(8,128)(2,1)S(1)}, u32[]{:S(2)}, u32[]{:S(2)}) collective-permute-start(bf16[80,2304]{1,0:T(8,128)(2,1)S(1)} %slice.3), channel_id=1, source_target_pairs={{0,4},{4,0},{1,5},{5,1},{2,6},{6,2},{3,7},{7,3}} | collective-permute-start | bytes 1105928 | tf_op jit(solution)/shard_map/ppermute | solution.py:363
  2.7 5.2 %copy_bitcast_fusion.1 = (bf16[2,2304,256]{2,1,0:T(8,128)(2,1)}, bf16[2,2304,256]{2,1,0:T(8,128)(2,1)}) fusion(bf16[2304,2,256]{2,1,0:T(2,128)(2,1)} %param.8, bf16[2304,2,256]{2,1,0:T(2,128)(2,1)} %param.7), kind=kLoop, calls=%fused_computation.1 | loop fusion | bytes 9437184 | tf_op jit(solution)/shard_map/transpose | solution.py:366
  7.9 0.0 slice-done
  7.9 0.0 slice-done.1
  7.9 2.7 %copy.12 = bf16[2304,4,256]{2,0,1:T(8,128)(2,1)} copy(bf16[2304,4,256]{2,1,0:T(4,128)(2,1)S(1)} %bitcast.9) | data formatting | bytes 9437184 | tf_op args[1]
  10.7 0.9 collective-permute-done.x_head_ref
  11.5 0.0 copy-start
  11.5 0.7 copy-done
  12.3 136.7 %attn_block.1 = bf16[768,2304]{1,0:T(8,128)(2,1)S(1)} custom-call(bf16[768,2304]{1,0:T(8,128)(2,1)} %x_ref.1, bf16[80,2304]{1,0:T(8,128)(2,1)} %copy-done, bf16[4,2304,256]{2,1,0:T(8,128)(2,1)} %bitcast.7, bf16[2,2304,256]{2,1,0:T(8,128)(2,1)} %get-tuple-element.6.wk_ref, bf16[2,2304,256]{2,1,0:T(8,128)(2,1)} %get-tuple-element.5.wv_ref, ...), custom_call_target="tpu_custom_call" | custom-call | tf_op jit(solution)/shard_map/attn_block/pallas_call | solution.py:368
  149.0 1.8 %copy.14 = bf16[768,2304]{1,0:T(8,128)(2,1)} copy(bf16[768,2304]{1,0:T(8,128)(2,1)S(1)} %attn_block.1) | data formatting | bytes 7077888
  (1 shorter events, 0.0 us)
Async XLA Ops:
  0.0 7.9 %slice-start = ((s8[4718592]{0:T(1024)(128)(4,1)}), s8[4194304]{0:T(1024)(128)(4,1)S(1)}, s32[]{:S(2)}) async-start(s8[4718592]{0:T(1024)(128)(4,1)} %bitcast.8), calls=%async_computation | async-start | bytes 8388608
  1.2 6.8 %slice-start.1 = ((s8[4718592]{0:T(1024)(128)(4,1)}), s8[524288]{0:T(1024)(128)(4,1)S(1)}, s32[]{:S(2)}) async-start(s8[4718592]{0:T(1024)(128)(4,1)} %bitcast.8), calls=%async_computation.1 | async-start | bytes 1048576
  1.2 10.3 %collective-permute-start = (bf16[80,2304]{1,0:T(8,128)(2,1)S(1)}, bf16[80,2304]{1,0:T(8,128)(2,1)S(1)}, u32[]{:S(2)}, u32[]{:S(2)}) collective-permute-start(bf16[80,2304]{1,0:T(8,128)(2,1)S(1)} %slice.3), channel_id=1, source_target_pairs={{0,4},{4,0},{1,5},{5,1},{2,6},{6,2},{3,7},{7,3}} | collective-permute-start | bytes 1105928 | tf_op jit(solution)/shard_map/ppermute | solution.py:363
  11.5 0.7 copy-start
